TPU v7x, 32 devices: a whole 2x2x4 slice. The times are simulated.
32 devices in a mesh: group: 2 (over y), station: 4 (over z), tm: 2 (over x), chan: 2 (over core).
Axes of the slice: x: 2, y: 2, z: 4, core: 2. Of those that a mesh axis runs over, the one named last changes fastest.
Arguments:
- voltages: bfloat16 [8, 128, 2, 96, 256], P(('group', 'station'), 'chan', None, None, 'tm'), parts along dimension 0, may hold values from -6 to 6
- delays: int32 [8], P(('group', 'station')), parts along dimension 0, may hold values from 0 to 16, as said below
- tap_sets: int32 [8, 128], P(('group', 'station'), 'chan'), parts along dimension 0, may hold values from 0 to 15
- tap_table: bfloat16 [16, 16], replicated, may hold values from -1.5 to 1.5
- weights: bfloat16 [8, 128, 2, 96, 128], P(('group', 'station'), 'chan'), parts along dimension 0, may hold values from -0.3125 to 0.3125
Outputs:
- array_beams: bfloat16 [256, 2, 128, 256], P(('group', 'chan', 'station'), None, None, 'tm'), parts along dimension 0
There are 2 independent parts, one for each index of `group`. A program takes and returns all parts, laid end to end along the dimension named above; an argument that names none is the same for every part. Nothing has to cross between parts.
Inputs may be any that keep to these rules, and one draw needn't show every extreme that they name: `delays`: every delay lies in 0 to 16, and some station has delay 16.
All inputs are finite; a program needn't handle non-finite values.
Results may differ from a plain program's by a relative error of at most 0.0049.
Values may be sent and summed in bfloat16 or wider, within the bound.
A program may use at most 64 MiB of HBM per device.

v0:
```python
import jax
import jax.numpy as jnp
from jax import lax
from jax.sharding import PartitionSpec as P

TAPS = 16
MAXD = 16
BLOCK = 128


def passed_along(value, axis, steps):
    count = lax.axis_size(axis)
    leading, last = (max(0, -steps), min(count, count - steps))
    return lax.ppermute(value, axis, [(source, source + steps) for source in range(leading, last)])


def steering_matrix(weights):
    real_w = weights[:, :, 0]
    imag_w = weights[:, :, 1]
    upper_rows = jnp.concatenate([real_w, imag_w], axis=-1)
    lower_rows = jnp.concatenate([-imag_w, real_w], axis=-1)
    return jnp.concatenate([upper_rows, lower_rows], axis=2)


def body(voltages, delays, tap_sets, tap_table, weights):
    station_number, channel_total, pairing_total, antenna_total, time_length = voltages.shape
    set_count, tap_count = tap_table.shape
    halo_len = MAXD + TAPS - 1
    window_len = BLOCK + halo_len
    flat_voltages = voltages.reshape(
        station_number, channel_total, pairing_total * antenna_total, time_length
    )
    prev_rim = passed_along(flat_voltages[..., time_length - halo_len :], "tm", 1)
    extended = jnp.concatenate([prev_rim, flat_voltages], axis=-1)
    windows = jnp.stack([extended], axis=3)
    set_onehot = (tap_sets[..., None] == jnp.arange(set_count)[None, None, :]).astype(jnp.bfloat16)
    chosen_taps = jnp.einsum(
        "scm,mk->sck", set_onehot, tap_table, preferred_element_type=jnp.float32
    ).astype(jnp.bfloat16)
    window_pos = jnp.arange(window_len)[:, None]
    output_pos = jnp.arange(BLOCK)[None, :]
    lag_table = output_pos + halo_len - window_pos
    station_lag = lag_table[None, :, :] - delays[:, None, None]
    tap_onehot = (station_lag[..., None] == jnp.arange(tap_count)[None, None, None, :]).astype(
        jnp.bfloat16
    )
    band_matrix = jnp.einsum(
        "sck,sjuk->scju", chosen_taps, tap_onehot, preferred_element_type=jnp.float32
    ).astype(jnp.bfloat16)
    delayed_voltages = jnp.einsum(
        "scanj,scju->scanu", windows, band_matrix, preferred_element_type=jnp.float32
    ).astype(jnp.bfloat16)
    delayed_voltages = delayed_voltages.reshape(
        station_number, channel_total, pairing_total * antenna_total, time_length
    )
    station_axis_size = lax.axis_size("station")
    row_count = channel_total // station_axis_size
    split_in = delayed_voltages.reshape(
        station_number, station_axis_size, row_count, pairing_total * antenna_total, time_length
    )
    split_steer = weights.reshape(
        station_number,
        station_axis_size,
        row_count,
        pairing_total,
        antenna_total,
        weights.shape[-1],
    )
    gathered_in = lax.all_to_all(split_in, "station", split_axis=1, concat_axis=0, tiled=True)
    gathered_w = lax.all_to_all(split_steer, "station", split_axis=1, concat_axis=0, tiled=True)
    summed = jnp.einsum(
        "scan,scat->cnt",
        steering_matrix(gathered_w[:, 0]),
        gathered_in[:, 0],
        preferred_element_type=jnp.float32,
    )
    beam_count = weights.shape[-1]
    return summed.astype(jnp.bfloat16).reshape(row_count, 2, beam_count, time_length)


def solution(mesh):
    return jax.shard_map(
        body,
        mesh=mesh,
        in_specs=(
            P(("group", "station"), "chan", None, None, "tm"),
            P(("group", "station")),
            P(("group", "station"), "chan"),
            P(),
            P(("group", "station"), "chan", None, None, None),
        ),
        out_specs=P(("group", "chan", "station"), None, None, "tm"),
        check_vma=False,
    )
```

profile of v0, /device:TPU:0, one launch (start us, length us, event | category | flops | bytes accessed | tf_op | source)
XLA Modules:
  0.0 160.1 jit_solution(11267425315163392430)
XLA Ops:
  0.0 0.0 copy-start
  0.0 3.9 %copy.12 = bf16[1,4,16,2,96,128]{5,4,2,3,0,1:T(8,128)(2,1)} copy(bf16[1,4,16,2,96,128]{5,4,3,2,1,0:T(8,128)(2,1)} %bitcast.40) | data formatting | bytes 6291456 | tf_op jit(solution)/shard_map/reshape | solution.py:61
  3.9 0.0 copy-start.1
  3.9 6.6 %all-to-all-start = ((bf16[1,4,16,2,96,128]{5,4,2,3,0,1:T(8,128)(2,1)}), bf16[1,4,16,2,96,128]{5,4,2,3,0,1:T(8,128)(2,1)}, u32[]{:S(2)}, u32[]{:S(2)}) async-start(bf16[1,4,16,2,96,128]{5,4,2,3,0,1:T(8,128)(2,1)} %copy.12), calls=%async_computation | async-start | bytes 6291456 | tf_op jit(solution)/shard_map/all_to_all | solution.py:70
  10.5 0.0 copy-done.1
  10.6 2.6 %slice.14 = bf16[1,64,192,31]{3,2,1,0:T(8,128)(2,1)} slice(bf16[1,64,192,128]{3,2,1,0:T(8,128)(2,1)S(1)} %bitcast.38), slice={[0:1], [0:64], [0:192], [97:128]} | slice | bytes 1523712 | tf_op jit(solution)/shard_map/slice | solution.py:33
  13.2 4.4 %copy.14 = bf16[1,64,192,31]{2,1,3,0:T(8,128)(2,1)} copy(bf16[1,64,192,31]{3,2,1,0:T(8,128)(2,1)} %slice.14) | data formatting | bytes 1523712 | tf_op jit(solution)/shard_map/slice | solution.py:33
  17.6 0.0 copy-start.2
  17.6 4.5 %collective-permute-start = (bf16[1,64,192,31]{2,1,3,0:T(8,128)(2,1)}, bf16[1,64,192,31]{2,1,3,0:T(8,128)(2,1)}, u32[]{:S(2)}, u32[]{:S(2)}) collective-permute-start(bf16[1,64,192,31]{2,1,3,0:T(8,128)(2,1)} %copy.14), channel_id=1, source_target_pairs={{0,2},{1,3},{4,6},{5,7},{8,10},{9,11},{12,14},{13,15},{16,18},{17,... | collective-permute-start | bytes 2285576 | tf_op jit(solution)/shard_map/ppermute | solution.py:14
  22.1 4.8 %copy.16 = bf16[1,64,192,128]{2,3,1,0:T(8,128)(2,1)} copy(bf16[1,64,192,128]{3,2,1,0:T(8,128)(2,1)S(1)} %bitcast.39) | data formatting | bytes 6291456 | tf_op jit(solution)/shard_map/reshape | solution.py:30
  27.6 0.0 copy-done
  27.6 0.0 copy-done.2
  27.6 1.1 convolution_convert_fusion
  28.7 14.2 %collective-permute-done = bf16[1,64,192,31]{2,1,3,0:T(8,128)(2,1)} collective-permute-done((bf16[1,64,192,31]{2,1,3,0:T(8,128)(2,1)}, bf16[1,64,192,31]{2,1,3,0:T(8,128)(2,1)}, u32[]{:S(2)}, u32[]{:S(2)}) %collective-permute-start) | collective-permute-done | bytes 761888 | tf_op jit(solution)/shard_map/ppermute | solution.py:14
  42.9 1.8 %copy.15 = bf16[1,64,192,31]{2,3,1,0:T(8,128)(2,1)S(1)} copy(bf16[1,64,192,31]{2,1,3,0:T(8,128)(2,1)} %collective-permute-done) | data formatting | bytes 1523712 | tf_op jit(solution)/shard_map/ppermute | solution.py:14
  44.7 8.7 %fusion.14 = bf16[64,192,128]{2,1,0:T(8,128)(2,1)} fusion(bf16[64,159,128]{2,0,1:T(8,128)(2,1)S(1)} %convolution_convert_fusion, bf16[1,64,192,128]{2,3,1,0:T(8,128)(2,1)} %copy.16, bf16[1,64,192,31]{2,3,1,0:T(8,128)(2,1)S(1)} %copy.15), kind=kOutput, calls=%fused_computation.16 | convolution fusion | flops 509558784 | bytes 9658368 | tf_op jit(solution)/shard_map/scanj,scju->scanu/dot_general | solution.py:50
  53.4 27.9 %all-to-all-done = bf16[1,4,16,2,96,128]{5,4,2,3,0,1:T(8,128)(2,1)} async-done(((bf16[1,4,16,2,96,128]{5,4,2,3,0,1:T(8,128)(2,1)}), bf16[1,4,16,2,96,128]{5,4,2,3,0,1:T(8,128)(2,1)}, u32[]{:S(2)}, u32[]{:S(2)}) %all-to-all-start) | async-done | bytes 3145760 | tf_op jit(solution)/shard_map/all_to_all | solution.py:70
  81.3 3.7 %all-to-all-start.1 = ((bf16[1,4,16,192,128]{4,3,2,0,1:T(8,128)(2,1)}), bf16[1,4,16,192,128]{4,3,2,0,1:T(8,128)(2,1)S(1)}, u32[]{:S(2)}, u32[]{:S(2)}) async-start(bf16[1,4,16,192,128]{4,3,2,0,1:T(8,128)(2,1)} %bitcast.10), calls=%async_computation.1 | async-start | bytes 6291456 | tf_op jit(solution)/shard_map/all_to_all | solution.py:69
  85.0 2.3 %copy.32 = bf16[1,4,16,2,96,128]{5,4,1,2,3,0:T(8,128)(2,1)S(1)} copy(bf16[1,4,16,2,96,128]{5,4,2,3,0,1:T(8,128)(2,1)} %all-to-all-done) | data formatting | bytes 6291456 | tf_op jit(solution)/shard_map/all_to_all | solution.py:70
  87.3 1.4 fusion.27
  88.7 2.0 %slice_bitcast_fusion = (bf16[4,16,96,128]{3,2,0,1:T(8,128)(2,1)}, bf16[4,16,96,128]{3,2,0,1:T(8,128)(2,1)}) fusion(bf16[4,16,2,96,128]{4,3,0,1,2:T(8,128)(2,1)S(1)} %bitcast.37), kind=kLoop, calls=%fused_computation.19 | loop fusion | bytes 6291456 | tf_op jit(solution)/shard_map/squeeze | solution.py:19
  90.7 64.4 %all-to-all-done.1 = bf16[1,4,16,192,128]{4,3,2,0,1:T(8,128)(2,1)S(1)} async-done(((bf16[1,4,16,192,128]{4,3,2,0,1:T(8,128)(2,1)}), bf16[1,4,16,192,128]{4,3,2,0,1:T(8,128)(2,1)S(1)}, u32[]{:S(2)}, u32[]{:S(2)}) %all-to-all-start.1) | async-done | bytes 3145760 | tf_op jit(solution)/shard_map/all_to_all | solution.py:69
  155.1 4.9 %bitcast_convert_fusion = bf16[16,256,128]{2,1,0:T(8,128)(2,1)} fusion(bf16[1,4,16,192,128]{4,3,2,0,1:T(8,128)(2,1)S(1)} %all-to-all-done.1, bf16[4,16,96,128]{3,2,0,1:T(8,128)(2,1)} %get-tuple-element.6, bf16[4,16,96,128]{3,2,0,1:T(8,128)(2,1)} %fusion.27, bf16[4,16,96,128]{3,2,0,1:T(8,128)(2,1)} %get-tuple-element.5), kind=kOutput, calls=%fused_computation.17 | convolution fusion | flops 830996480 | bytes 8912896 | tf_op jit(solution)/shard_map/scan,scat->cnt/dot_general | solution.py:71
  (2 shorter events, 0.0 us)
Async XLA Ops:
  0.0 27.6 %copy-start = (bf16[16,16]{1,0:T(8,128)(2,1)S(1)}, bf16[16,16]{1,0:T(8,128)(2,1)}, u32[]{:S(2)}) copy-start(bf16[16,16]{1,0:T(8,128)(2,1)} %param.8) | copy-start | bytes 1540
  3.9 6.6 %copy-start.1 = (bf16[1,64,2,96,128]{4,3,2,1,0:T(8,128)(2,1)S(1)}, bf16[1,64,2,96,128]{4,3,2,1,0:T(8,128)(2,1)}, u32[]{:S(2)}) copy-start(bf16[1,64,2,96,128]{4,3,2,1,0:T(8,128)(2,1)} %param.5) | copy-start | bytes 9437188
  3.9 77.4 %all-to-all-start = ((bf16[1,4,16,2,96,128]{5,4,2,3,0,1:T(8,128)(2,1)}), bf16[1,4,16,2,96,128]{5,4,2,3,0,1:T(8,128)(2,1)}, u32[]{:S(2)}, u32[]{:S(2)}) async-start(bf16[1,4,16,2,96,128]{5,4,2,3,0,1:T(8,128)(2,1)} %copy.12), calls=%async_computation | async-start | bytes 6291456 | tf_op jit(solution)/shard_map/all_to_all | solution.py:70
  17.6 10.0 %copy-start.2 = (s32[1,64]{1,0:T(1,128)S(1)}, s32[1,64]{1,0:T(1,128)}, u32[]{:S(2)}) copy-start(s32[1,64]{1,0:T(1,128)} %param.7) | copy-start | bytes 772
  17.6 25.3 %collective-permute-start = (bf16[1,64,192,31]{2,1,3,0:T(8,128)(2,1)}, bf16[1,64,192,31]{2,1,3,0:T(8,128)(2,1)}, u32[]{:S(2)}, u32[]{:S(2)}) collective-permute-start(bf16[1,64,192,31]{2,1,3,0:T(8,128)(2,1)} %copy.14), channel_id=1, source_target_pairs={{0,2},{1,3},{4,6},{5,7},{8,10},{9,11},{12,14},{13,15},{16,18},{17,... | collective-permute-start | bytes 2285576 | tf_op jit(solution)/shard_map/ppermute | solution.py:14
  81.3 73.8 %all-to-all-start.1 = ((bf16[1,4,16,192,128]{4,3,2,0,1:T(8,128)(2,1)}), bf16[1,4,16,192,128]{4,3,2,0,1:T(8,128)(2,1)S(1)}, u32[]{:S(2)}, u32[]{:S(2)}) async-start(bf16[1,4,16,192,128]{4,3,2,0,1:T(8,128)(2,1)} %bitcast.10), calls=%async_computation.1 | async-start | bytes 6291456 | tf_op jit(solution)/shard_map/all_to_all | solution.py:69
where the time goes:
time: 161 us; the launch traced here: 160 us
  waiting for transfers between devices  107 us (66%)
  local copies, waits for them, and re-layouts  21.9 us (14%)
  starting transfers between devices  14.8 us (9%)
  matrix products  14.7 us (9%)
    all_to_all x1, waiting for transfers between devices, body(): lax.all_to_all(split_in, 'station', split_axis=1, concat_axis=0, tiled=True)  64.4 us
    all_to_all x1, waiting for transfers between devices, body(): lax.all_to_all(split_steer, 'station', split_axis=1, concat_axis=0, tiled...  27.9 us
    ppermute x1, waiting for transfers between devices, passed_along(): lax.ppermute(value, axis, [(source, source + steps) for source in range(l...  14.2 us
    dot_general x1, matrix products, body(): jnp.einsum('scanj,scju->scanu', windows, band_matrix, preferred_element_t...  8.68 us
    slice x2, local copies, waits for them, and re-layouts, body(): flat_voltages[..., time_length - halo_len:]  7.05 us
    all_to_all x1, starting transfers between devices, body(): lax.all_to_all(split_steer, 'station', split_axis=1, concat_axis=0, tiled...  6.61 us
    dot_general x1, matrix products, body(): jnp.einsum('scan,scat->cnt', steering_matrix(gathered_w[:, 0]), gathered_...  4.93 us
    reshape x1, local copies, waits for them, and re-layouts, body(): voltages.reshape(station_number, channel_total, pairing_total * antenna_t...  4.84 us
  transfers between devices with their start and end apart: 3, of which 3 were waited for; matrix products, arithmetic and copies ran while one was open for 18% of the time, Pallas kernels for 0%

commit v1 on v0

--- a/solution.py
+++ b/solution.py
@@ -2,10 +2,23 @@
 import jax.numpy as jnp
 from jax import lax
 from jax.sharding import PartitionSpec as P
+from jax.lax import all_to_all, axis_size
 
 TAPS = 16
 MAXD = 16
 BLOCK = 128
+
+
+def change_the_classes(my_data, mesh_dim):
+    return jnp.concatenate(
+        all_to_all(
+            jnp.stack(jnp.split(my_data, axis_size(mesh_dim), axis=1)),
+            axis_name=mesh_dim,
+            split_axis=0,
+            concat_axis=0,
+        ),
+        axis=0,
+    )
 
 
 def passed_along(value, axis, steps):
@@ -67,7 +80,7 @@
         weights.shape[-1],
     )
     gathered_in = lax.all_to_all(split_in, "station", split_axis=1, concat_axis=0, tiled=True)
-    gathered_w = lax.all_to_all(split_steer, "station", split_axis=1, concat_axis=0, tiled=True)
+    gathered_w = change_the_classes(split_steer, "station")
     summed = jnp.einsum(
         "scan,scat->cnt",
         steering_matrix(gathered_w[:, 0]),

time: 161 us -> 161 us (level)
    another operation x0 -> x2, local copies, waits for them, and re-layouts: none -> 4.08 us  [change_the_classes(): jnp.stack(jnp.split(my_data, axis_size(mesh_dim), axis=1))]
    reshape x1 -> x0, local copies, waits for them, and re-layouts: 3.93 us -> none  [body(): weights.reshape(station_number, station_axis_size, row_count, pairing_tot...]
where the time goes in v1:
time: 161 us
  waiting for transfers between devices  107 us (66%)
  local copies, waits for them, and re-layouts  22.1 us (14%)
  starting transfers between devices  14.8 us (9%)
  matrix products  14.7 us (9%)
  other arithmetic  1.83 us (1%)
    all_to_all x1, waiting for transfers between devices, body(): lax.all_to_all(split_in, 'station', split_axis=1, concat_axis=0, tiled=True)  64.4 us
    all_to_all x1, waiting for transfers between devices, change_the_classes(): all_to_all(jnp.stack(jnp.split(my_data, axis_size(mesh_dim), axis=1)), ax...  27.9 us
    ppermute x1, waiting for transfers between devices, passed_along(): lax.ppermute(value, axis, [(source, source + steps) for source in range(l...  14.2 us
    dot_general x1, matrix products, body(): jnp.einsum('scanj,scju->scanu', windows, band_matrix, preferred_element_t...  8.69 us
    slice x2, local copies, waits for them, and re-layouts, body(): flat_voltages[..., time_length - halo_len:]  7.05 us
    all_to_all x1, starting transfers between devices, change_the_classes(): all_to_all(jnp.stack(jnp.split(my_data, axis_size(mesh_dim), axis=1)), ax...  6.61 us
    dot_general x1, matrix products, body(): jnp.einsum('scan,scat->cnt', steering_matrix(gathered_w[:, 0]), gathered_...  4.93 us
    reshape x1, local copies, waits for them, and re-layouts, body(): voltages.reshape(station_number, channel_total, pairing_total * antenna_t...  4.87 us
  transfers between devices with their start and end apart: 3, of which 3 were waited for; matrix products, arithmetic and copies ran while one was open for 18% of the time, Pallas kernels for 0%

profile of v1, /device:TPU:0, one launch (start us, length us, event | category | flops | bytes accessed | tf_op | source)
XLA Modules:
  0.0 160.7 jit_solution(4297086752229704053)
XLA Ops:
  0.0 0.0 copy-start
  0.0 2.1 %slice_bitcast_fusion.5 = (bf16[1,1,1,16,2,96,128]{6,5,4,3,2,1,0:T(8,128)(2,1)S(1)}, bf16[1,1,1,16,2,96,128]{6,5,4,3,2,1,0:T(8,128)(2,1)S(1)}, bf16[1,1,1,16,2,9...) fusion(bf16[1,4,16,2,96,128]{5,4,3,2,1,0:T(8,128)(2,1)} %bitcast.48), kind=kLoop, calls=%fused_computation.28 | loop fusion | bytes 6291456 | tf_op jit(solution)/shard_map/stack | solution.py:15
  2.1 0.4 pad_maximum_fusion
  2.5 2.0 %copy.18 = bf16[4,1,1,16,2,96,128]{6,5,3,4,2,1,0:T(8,128)(2,1)} copy(bf16[4,1,1,16,2,96,128]{6,5,4,3,2,1,0:T(8,128)(2,1)S(1)} %pad_maximum_fusion) | data formatting | bytes 6291456 | tf_op jit(solution)/shard_map/stack | solution.py:15
  4.5 0.0 copy-start.1
  4.5 6.6 %all-to-all-start = ((bf16[4,1,1,16,2,96,128]{6,5,3,4,2,1,0:T(8,128)(2,1)}), bf16[4,1,1,16,2,96,128]{6,5,3,4,2,1,0:T(8,128)(2,1)}, u32[]{:S(2)}, u32[]{:S(2)}) async-start(bf16[4,1,1,16,2,96,128]{6,5,3,4,2,1,0:T(8,128)(2,1)} %copy.18), calls=%async_computation | async-start | bytes 6291456 | tf_op jit(solution)/shard_map/all_to_all | solution.py:14
  11.2 0.0 copy-done.1
  11.2 2.6 %slice.14 = bf16[1,64,192,31]{3,2,1,0:T(8,128)(2,1)} slice(bf16[1,64,192,128]{3,2,1,0:T(8,128)(2,1)S(1)} %bitcast.46), slice={[0:1], [0:64], [0:192], [97:128]} | slice | bytes 1523712 | tf_op jit(solution)/shard_map/slice | solution.py:46
  13.8 4.4 %copy.20 = bf16[1,64,192,31]{2,1,3,0:T(8,128)(2,1)} copy(bf16[1,64,192,31]{3,2,1,0:T(8,128)(2,1)} %slice.14) | data formatting | bytes 1523712 | tf_op jit(solution)/shard_map/slice | solution.py:46
  18.2 0.0 copy-start.2
  18.2 4.5 %collective-permute-start = (bf16[1,64,192,31]{2,1,3,0:T(8,128)(2,1)}, bf16[1,64,192,31]{2,1,3,0:T(8,128)(2,1)}, u32[]{:S(2)}, u32[]{:S(2)}) collective-permute-start(bf16[1,64,192,31]{2,1,3,0:T(8,128)(2,1)} %copy.20), channel_id=1, source_target_pairs={{0,2},{1,3},{4,6},{5,7},{8,10},{9,11},{12,14},{13,15},{16,18},{17,... | collective-permute-start | bytes 2285576 | tf_op jit(solution)/shard_map/ppermute | solution.py:27
  22.7 4.9 %copy.22 = bf16[1,64,192,128]{2,3,1,0:T(8,128)(2,1)} copy(bf16[1,64,192,128]{3,2,1,0:T(8,128)(2,1)S(1)} %bitcast.47) | data formatting | bytes 6291456 | tf_op jit(solution)/shard_map/reshape | solution.py:43
  28.3 0.0 copy-done
  28.3 0.0 copy-done.2
  28.3 1.1 convolution_convert_fusion
  29.4 14.2 %collective-permute-done = bf16[1,64,192,31]{2,1,3,0:T(8,128)(2,1)} collective-permute-done((bf16[1,64,192,31]{2,1,3,0:T(8,128)(2,1)}, bf16[1,64,192,31]{2,1,3,0:T(8,128)(2,1)}, u32[]{:S(2)}, u32[]{:S(2)}) %collective-permute-start) | collective-permute-done | bytes 761888 | tf_op jit(solution)/shard_map/ppermute | solution.py:27
  43.5 1.8 %copy.21 = bf16[1,64,192,31]{2,3,1,0:T(8,128)(2,1)S(1)} copy(bf16[1,64,192,31]{2,1,3,0:T(8,128)(2,1)} %collective-permute-done) | data formatting | bytes 1523712 | tf_op jit(solution)/shard_map/ppermute | solution.py:27
  45.3 8.7 %fusion.14 = bf16[64,192,128]{2,1,0:T(8,128)(2,1)} fusion(bf16[64,159,128]{2,0,1:T(8,128)(2,1)S(1)} %convolution_convert_fusion, bf16[1,64,192,128]{2,3,1,0:T(8,128)(2,1)} %copy.22, bf16[1,64,192,31]{2,3,1,0:T(8,128)(2,1)S(1)} %copy.21), kind=kOutput, calls=%fused_computation.17 | convolution fusion | flops 509558784 | bytes 9658368 | tf_op jit(solution)/shard_map/scanj,scju->scanu/dot_general | solution.py:63
  54.0 27.9 %all-to-all-done = bf16[4,1,1,16,2,96,128]{6,5,3,4,2,1,0:T(8,128)(2,1)} async-done(((bf16[4,1,1,16,2,96,128]{6,5,3,4,2,1,0:T(8,128)(2,1)}), bf16[4,1,1,16,2,96,128]{6,5,3,4,2,1,0:T(8,128)(2,1)}, u32[]{:S(2)}, u32[]{:S(2)}) %all-to-all-start) | async-done | bytes 3145760 | tf_op jit(solution)/shard_map/all_to_all | solution.py:14
  81.9 3.7 %all-to-all-start.1 = ((bf16[1,4,16,192,128]{4,3,2,0,1:T(8,128)(2,1)}), bf16[1,4,16,192,128]{4,3,2,0,1:T(8,128)(2,1)S(1)}, u32[]{:S(2)}, u32[]{:S(2)}) async-start(bf16[1,4,16,192,128]{4,3,2,0,1:T(8,128)(2,1)} %bitcast.14), calls=%async_computation.1 | async-start | bytes 6291456 | tf_op jit(solution)/shard_map/all_to_all | solution.py:82
  85.6 2.3 %copy.38 = bf16[4,1,1,16,2,96,128]{6,5,0,3,4,2,1:T(8,128)(2,1)S(1)} copy(bf16[4,1,1,16,2,96,128]{6,5,3,4,2,1,0:T(8,128)(2,1)} %all-to-all-done) | data formatting | bytes 6291456 | tf_op jit(solution)/shard_map/all_to_all | solution.py:14
  87.9 1.4 fusion.27
  89.3 2.0 %slice_bitcast_fusion = (bf16[4,16,96,128]{3,2,0,1:T(8,128)(2,1)}, bf16[4,16,96,128]{3,2,0,1:T(8,128)(2,1)}) fusion(bf16[4,16,2,96,128]{4,3,0,1,2:T(8,128)(2,1)S(1)} %bitcast.45), kind=kLoop, calls=%fused_computation.20 | loop fusion | bytes 6291456 | tf_op jit(solution)/shard_map/squeeze | solution.py:32
  91.3 64.4 %all-to-all-done.1 = bf16[1,4,16,192,128]{4,3,2,0,1:T(8,128)(2,1)S(1)} async-done(((bf16[1,4,16,192,128]{4,3,2,0,1:T(8,128)(2,1)}), bf16[1,4,16,192,128]{4,3,2,0,1:T(8,128)(2,1)S(1)}, u32[]{:S(2)}, u32[]{:S(2)}) %all-to-all-start.1) | async-done | bytes 3145760 | tf_op jit(solution)/shard_map/all_to_all | solution.py:82
  155.7 4.9 %bitcast_convert_fusion = bf16[16,256,128]{2,1,0:T(8,128)(2,1)} fusion(bf16[1,4,16,192,128]{4,3,2,0,1:T(8,128)(2,1)S(1)} %all-to-all-done.1, bf16[4,16,96,128]{3,2,0,1:T(8,128)(2,1)} %get-tuple-element.6, bf16[4,16,96,128]{3,2,0,1:T(8,128)(2,1)} %fusion.27, bf16[4,16,96,128]{3,2,0,1:T(8,128)(2,1)} %get-tuple-element.5), kind=kOutput, calls=%fused_computation.18 | convolution fusion | flops 830996480 | bytes 8912896 | tf_op jit(solution)/shard_map/scan,scat->cnt/dot_general | solution.py:84
  (2 shorter events, 0.0 us)
Async XLA Ops:
  0.0 28.3 %copy-start = (bf16[16,16]{1,0:T(8,128)(2,1)S(1)}, bf16[16,16]{1,0:T(8,128)(2,1)}, u32[]{:S(2)}) copy-start(bf16[16,16]{1,0:T(8,128)(2,1)} %param.8) | copy-start | bytes 1540
  4.5 6.6 %copy-start.1 = (bf16[1,64,2,96,128]{4,3,2,1,0:T(8,128)(2,1)S(1)}, bf16[1,64,2,96,128]{4,3,2,1,0:T(8,128)(2,1)}, u32[]{:S(2)}) copy-start(bf16[1,64,2,96,128]{4,3,2,1,0:T(8,128)(2,1)} %param.5) | copy-start | bytes 9437188
  4.5 77.4 %all-to-all-start = ((bf16[4,1,1,16,2,96,128]{6,5,3,4,2,1,0:T(8,128)(2,1)}), bf16[4,1,1,16,2,96,128]{6,5,3,4,2,1,0:T(8,128)(2,1)}, u32[]{:S(2)}, u32[]{:S(2)}) async-start(bf16[4,1,1,16,2,96,128]{6,5,3,4,2,1,0:T(8,128)(2,1)} %copy.18), calls=%async_computation | async-start | bytes 6291456 | tf_op jit(solution)/shard_map/all_to_all | solution.py:14
  18.2 10.1 %copy-start.2 = (s32[1,64]{1,0:T(1,128)S(1)}, s32[1,64]{1,0:T(1,128)}, u32[]{:S(2)}) copy-start(s32[1,64]{1,0:T(1,128)} %param.7) | copy-start | bytes 772
  18.2 25.3 %collective-permute-start = (bf16[1,64,192,31]{2,1,3,0:T(8,128)(2,1)}, bf16[1,64,192,31]{2,1,3,0:T(8,128)(2,1)}, u32[]{:S(2)}, u32[]{:S(2)}) collective-permute-start(bf16[1,64,192,31]{2,1,3,0:T(8,128)(2,1)} %copy.20), channel_id=1, source_target_pairs={{0,2},{1,3},{4,6},{5,7},{8,10},{9,11},{12,14},{13,15},{16,18},{17,... | collective-permute-start | bytes 2285576 | tf_op jit(solution)/shard_map/ppermute | solution.py:27
  81.9 73.8 %all-to-all-start.1 = ((bf16[1,4,16,192,128]{4,3,2,0,1:T(8,128)(2,1)}), bf16[1,4,16,192,128]{4,3,2,0,1:T(8,128)(2,1)S(1)}, u32[]{:S(2)}, u32[]{:S(2)}) async-start(bf16[1,4,16,192,128]{4,3,2,0,1:T(8,128)(2,1)} %bitcast.14), calls=%async_computation.1 | async-start | bytes 6291456 | tf_op jit(solution)/shard_map/all_to_all | solution.py:82
